TPU v7x, 32 devices: a whole 2x2x4 slice. The times are simulated.
32 devices in a mesh: wide: 8 (over z, x), narrow: 4 (over y, core).
Axes of the slice: x: 2, y: 2, z: 4, core: 2. Of those that a mesh axis runs over, the one named last changes fastest.
Arguments:
- activations: bfloat16 [2048, 16384], P('wide', 'narrow'), may hold values from -6 to 6
- grad_out: bfloat16 [2048, 8192], P('narrow', 'wide'), may hold values from -0.125 to 0.125
- momentum: float32 [8192, 16384], P('wide', 'narrow'), may hold values from -90 to 90
- right_factor: float32 [16384, 512], P('narrow'), may hold values from -0.046875 to 0.046875
Outputs:
- new_momentum: float32 [8192, 16384], P('wide', 'narrow')
- new_right: float32 [16384, 512], P('narrow')
- update: bfloat16 [8192, 16384], P('wide', 'narrow')
All inputs are finite; a program needn't handle non-finite values.
Results may differ from a plain program's by a relative error of at most 0.0012.
Values may be sent and summed in bfloat16 or wider, within the bound.
No kernel may reach another device: no remote copies, remote signals or barrier semaphores. Data moves between devices by JAX's collectives and lax.ppermute only.
A program may use at most 128 MiB of HBM per device.

v0:
```python
import math
import jax
import jax.numpy as jnp
from jax import lax
from jax.sharding import PartitionSpec as P

DOUT = 8192
DIN = 16384
RANK = 512
FEEDBACK = 0.05
EPSILON = 1e-06


def body(activations, grad_out, momentum, right_factor):
    highest = lax.Precision.HIGHEST
    out_rows = lax.all_gather(grad_out, "narrow", axis=0, tiled=True)
    gradient = lax.dot_general(
        out_rows,
        lax.all_gather(activations, "wide", axis=0, tiled=True),
        (((0,), (0,)), ((), ())),
        preferred_element_type=jnp.float32,
    )
    buffer = momentum + gradient
    partial_left = jnp.dot(
        buffer, right_factor, precision=highest, preferred_element_type=jnp.float32
    )
    left_factor = lax.psum(partial_left, "narrow")
    gram_local = jnp.dot(
        left_factor.T, left_factor, precision=highest, preferred_element_type=jnp.float32
    )
    gram_matrix = lax.psum(gram_local, "wide")
    lower_factor = jnp.linalg.cholesky(gram_matrix)
    ortho_left = jax.scipy.linalg.solve_triangular(lower_factor, left_factor.T, lower=True).T
    right_share = lax.psum_scatter(
        lax.dot_general(
            buffer,
            ortho_left,
            (((0,), (0,)), ((), ())),
            precision=highest,
            preferred_element_type=jnp.float32,
        ),
        "wide",
        scatter_dimension=0,
        tiled=True,
    )
    col_squares = lax.psum(jnp.sum(right_share * right_share, axis=0), ("wide", "narrow"))
    right_raw = lax.all_gather(right_share, "wide", axis=0, tiled=True)
    feedback = lax.dot_general(
        ortho_left,
        right_raw,
        (((1,), (1,)), ((), ())),
        precision=highest,
        preferred_element_type=jnp.float32,
    )
    new_momentum = buffer - FEEDBACK * feedback
    new_right = right_raw / (jnp.sqrt(col_squares) + EPSILON)
    update_scale = math.sqrt(DOUT * DIN / RANK)
    product = lax.dot_general(
        ortho_left,
        new_right,
        (((1,), (1,)), ((), ())),
        precision=highest,
        preferred_element_type=jnp.float32,
    )
    update = (update_scale * product).astype(jnp.bfloat16)
    return (new_momentum, new_right, update)


def solution(mesh):
    return jax.shard_map(
        body,
        mesh=mesh,
        in_specs=(P("wide", "narrow"), P("narrow", "wide"), P("wide", "narrow"), P("narrow", None)),
        out_specs=(P("wide", "narrow"), P("narrow", None), P("wide", "narrow")),
        check_vma=False,
    )
```

profile of v0, /device:TPU:0, one launch (start us, length us, event | category | flops | bytes accessed | tf_op | source)
XLA Modules:
  0.0 1089.3 jit_solution(18141778755275494876)
XLA Ops:
  8.7 38.1 %all-gather.4.cloned.1.call-done = bf16[2048,1024]{1,0:T(8,128)(2,1)} async-done(((bf16[512,1024]{1,0:T(8,128)(2,1)}), bf16[2048,1024]{1,0:T(8,128)(2,1)}) %all-gather.4.cloned.1.call-update) | async-done | bytes 4194320 | tf_op jit(solution)/shard_map/all_gather | solution.py:16
  46.7 229.4 %all-gather.6.cloned.1.call-done = bf16[2048,4096]{1,0:T(8,128)(2,1)} async-done(((bf16[256,4096]{1,0:T(8,128)(2,1)}), bf16[2048,4096]{1,0:T(8,128)(2,1)}) %all-gather.6.cloned.1.call-update) | async-done | bytes 16777232 | tf_op jit(solution)/shard_map/all_gather | solution.py:19
  276.2 28.3 %convolution_add_fusion = f32[1024,4096]{1,0:T(8,128)} fusion(f32[1024,4096]{1,0:T(8,128)} %param.6, bf16[2048,1024]{1,0:T(8,128)(2,1)} %all-gather.4.cloned.1.call-done, bf16[2048,4096]{1,0:T(8,128)(2,1)} %all-gather.6.cloned.1.call-done), kind=kOutput, calls=%fused_computation.4 | convolution fusion | flops 17184063488 | bytes 54525952 | tf_op jit(solution)/shard_map/dot_general | solution.py:17
  304.5 31.4 %fusion.39 = f32[1024,512]{1,0:T(8,128)} fusion(f32[1024,4096]{1,0:T(8,128)} %convolution_add_fusion, f32[4096,512]{1,0:T(8,128)} %param.7), kind=kOutput, calls=%fused_computation.78 | convolution fusion | flops 25769803776 | bytes 27262976 | tf_op jit(solution)/shard_map/dot_general | solution.py:24
  336.0 49.7 %all-reduce.4.cloned.1.call-done = f32[1024,512]{1,0:T(8,128)} async-done(((f32[1024,512]{1,0:T(8,128)}), f32[1024,512]{1,0:T(8,128)}) %all-reduce.4.cloned.1.call-update) | async-done | bytes 2097168 | tf_op jit(solution)/shard_map/psum | solution.py:27
  385.6 6.7 fusion.40
  392.6 78.3 %all-reduce.6.cloned.1.call-done = f32[512,512]{0,1:T(8,128)} async-done(((f32[512,512]{0,1:T(8,128)}), f32[512,512]{0,1:T(8,128)}) %all-reduce.6.cloned.1.call-update) | async-done | bytes 1048592 | tf_op jit(solution)/shard_map/psum | solution.py:31
  474.9 11.7 %cholesky.104 = f32[128,128]{1,0:T(8,128)S(1)} custom-call(f32[128,128]{1,0:T(8,128)S(1)} %cholesky.266), custom_call_target="Cholesky" | custom-call | tf_op jit(solution)/shard_map/jit(cholesky)/cholesky | solution.py:32
  486.8 9.8 custom-call.31
  499.1 11.7 %cholesky.217 = f32[128,128]{1,0:T(8,128)S(1)} custom-call(f32[128,128]{1,0:T(8,128)S(1)} %cholesky.270), custom_call_target="Cholesky" | custom-call | tf_op jit(solution)/shard_map/jit(cholesky)/cholesky | solution.py:32
  510.9 10.0 custom-call.32
  522.5 11.7 %cholesky.238 = f32[128,128]{1,0:T(8,128)S(1)} custom-call(f32[128,128]{1,0:T(8,128)S(1)} %cholesky.275), custom_call_target="Cholesky" | custom-call | tf_op jit(solution)/shard_map/jit(cholesky)/cholesky | solution.py:32
  534.2 9.8 custom-call.33
  545.5 11.7 %cholesky.255 = f32[128,128]{1,0:T(8,128)S(1)} custom-call(f32[128,128]{1,0:T(8,128)S(1)} %convolution_subtract_fusion.4), custom_call_target="Cholesky" | custom-call | tf_op jit(solution)/shard_map/jit(cholesky)/cholesky | solution.py:32
  563.3 13.6 %while.1 = (s32[]{:T(128)}, f32[512,512]{1,0:T(8,128)}, s32[4,2]{0,1:T(2,128)S(1)}, f32[4,128,128]{2,1,0:T(8,128)}, s32[]{:T(128)}) while((s32[]{:T(128)}, f32[512,512]{1,0:T(8,128)}, s32[4,2]{0,1:T(2,128)S(1)}, f32[4,128,128]{2,1,0:T(8,128)}, s32[]{:T(128)}) %tuple.31), condition=%wide.while_cond, body=%wide.while_body.sunk | while | flops 2 | bytes 132205 | solution.py:33
  576.9 40.1 %custom-call.34 = f32[4,128,128]{1,2,0:T(8,128)S(1)} custom-call(f32[4,128,128]{2,1,0:T(8,128)} %get-tuple-element.10), custom_call_target="InvertDiagBlocksLowerTriangular" | custom-call | tf_op jit(solution)/shard_map/jit(_solve_triangular)/triangular_solve | solution.py:33
  623.7 3.8 fusion.6
  629.0 56.3 %fusion.15 = f32[4096,512]{1,0:T(8,128)} fusion(f32[1024,4096]{1,0:T(8,128)} %convolution_add_fusion, f32[128,1024]{1,0:T(8,128)S(1)} %fusion.24, f32[128,1024]{1,0:T(8,128)S(1)} %fusion.25, f32[128,1024]{1,0:T(8,128)S(1)} %fusion.27, f32[128,1024]{1,0:T(8,128)S(1)} %fusion.13), kind=kOutput, calls=%fused_computation.31 | convolution fusion | flops 25771376640 | bytes 27262976 | tf_op jit(solution)/shard_map/dot_general | solution.py:35
  685.4 147.2 %reduce-scatter.2.cloned.1.call-done = f32[512,512]{1,0:T(8,128)} async-done(((f32[4096,512]{1,0:T(8,128)}), f32[512,512]{1,0:T(8,128)}) %reduce-scatter.2.cloned.1.call-update) | async-done | bytes 1048592 | tf_op jit(solution)/shard_map/reduce_scatter | solution.py:34
  833.9 43.3 %psum.23 = f32[512]{0:T(512)S(1)} all-reduce(f32[512]{0:T(512)S(1)} %multiply_reduce_fusion), channel_id=1, replica_groups=mesh['wide'=8,'narrow'=4] {'wide','narrow'}, use_global_device_ids=true, to_apply=%region_12.13 | all-reduce | flops 512 | bytes 4096 | tf_op jit(solution)/shard_map/psum | solution.py:46
  877.2 82.0 %all-gather.8.cloned.1.call-done = f32[4096,512]{1,0:T(8,128)} async-done(((f32[512,512]{1,0:T(8,128)}), f32[4096,512]{1,0:T(8,128)}) %all-gather.8.cloned.1.call-update) | async-done | bytes 8388624 | tf_op jit(solution)/shard_map/all_gather | solution.py:47
  959.2 8.9 broadcast_divide_fusion
  968.1 56.8 %multiply_convert_fusion = bf16[1024,4096]{1,0:T(8,128)(2,1)} fusion(f32[4096,512]{1,0:T(8,128)} %broadcast_divide_fusion, f32[128,1024]{1,0:T(8,128)} %copy-done.4, f32[128,1024]{1,0:T(8,128)} %copy-done.2, f32[128,1024]{1,0:T(8,128)} %copy-done.1, f32[128,1024]{1,0:T(8,128)S(1)} %fusion.13), kind=kOutput, calls=%fused_computation.2 | convolution fusion | flops 25779765248 | bytes 18874368 | tf_op jit(solution)/shard_map/dot_general | solution.py:58
  1025.0 57.3 %multiply_subtract_fusion = f32[1024,4096]{1,0:T(8,128)} fusion(f32[1024,4096]{1,0:T(8,128)S(1)} %bitcast.65, f32[4096,512]{1,0:T(8,128)S(1)} %bitcast.59, f32[128,1024]{1,0:T(8,128)} %copy-done.4, f32[128,1024]{1,0:T(8,128)} %copy-done.2, f32[128,1024]{1,0:T(8,128)} %copy-done.1, f32[128,1024]{1,0:T(8,128)S(1)} %fusion.13), kind=kOutput, calls=%fused_computation.3 | convolution fusion | flops 25779765248 | bytes 44040192 | tf_op jit(solution)/shard_map/dot_general | solution.py:48
  (79 shorter events, 38.1 us)
Async XLA Ops:
  7.2 39.6 %all-gather.4.cloned.1.call-start = ((), (), s32[]{:S(2)}) async-start(), calls=%async_computation.1 | async-start | bytes 5242880 | tf_op jit(solution)/shard_map/all_gather | solution.py:16
  7.9 268.3 %all-gather.6.cloned.1.call-start = ((), (), s32[]{:S(2)}) async-start(), calls=%async_computation.2 | async-start | bytes 18874368 | tf_op jit(solution)/shard_map/all_gather | solution.py:19
  8.6 377.0 %all-reduce.4.cloned.1.call-start = ((), (), s32[]{:S(2)}) async-start(), calls=%async_computation.3 | async-start | bytes 4194304 | tf_op jit(solution)/shard_map/psum | solution.py:27
  335.9 135.0 %all-reduce.6.cloned.1.call-start = ((), (), s32[]{:S(2)}) async-start(), calls=%async_computation.4 | async-start | bytes 2097152 | tf_op jit(solution)/shard_map/psum | solution.py:31
  392.4 440.2 %reduce-scatter.2.cloned.1.call-start = ((), (), s32[]{:S(2)}) async-start(), calls=%async_computation.5 | async-start | bytes 9437184 | tf_op jit(solution)/shard_map/reduce_scatter | solution.py:34
  473.9 1.0 copy-start.3
  474.9 142.1 %copy-start = (f32[1024,512]{1,0:T(8,128)S(1)}, f32[1024,512]{1,0:T(8,128)}, u32[]{:S(2)}) copy-start(f32[1024,512]{1,0:T(8,128)} %all-reduce.4.cloned.1.call-done) | copy-start | bytes 6291460
  620.2 65.1 %copy-start.1 = (f32[128,1024]{1,0:T(8,128)}, f32[128,1024]{1,0:T(8,128)S(1)}, u32[]{:S(2)}) copy-start(f32[128,1024]{1,0:T(8,128)S(1)} %fusion.27) | copy-start | bytes 1572868
  623.7 4.5 copy-start.2
  628.2 0.8 copy-start.4
  685.3 273.9 %all-gather.8.cloned.1.call-start = ((), (), s32[]{:S(2)}) async-start(), calls=%async_computation.6 | async-start | bytes 9437184 | tf_op jit(solution)/shard_map/all_gather | solution.py:47
  959.2 65.7 %slice-start = ((s8[8388608]{0:T(1024)(128)(4,1)}), s8[4194304]{0:T(1024)(128)(4,1)S(1)}, s32[]{:S(2)}) async-start(s8[8388608]{0:T(1024)(128)(4,1)} %bitcast.58), calls=%async_computation.7 | async-start | bytes 8388608
  959.2 65.7 %slice-start.2 = ((s8[16777216]{0:T(1024)(128)(4,1)}), s8[4194304]{0:T(1024)(128)(4,1)S(1)}, s32[]{:S(2)}) async-start(s8[16777216]{0:T(1024)(128)(4,1)} %bitcast.64), calls=%async_computation.9 | async-start | bytes 8388608
  959.2 65.7 %slice-start.3 = ((s8[16777216]{0:T(1024)(128)(4,1)}), s8[4194304]{0:T(1024)(128)(4,1)S(1)}, s32[]{:S(2)}) async-start(s8[16777216]{0:T(1024)(128)(4,1)} %bitcast.64), calls=%async_computation.10 | async-start | bytes 8388608
  968.1 56.8 %slice-start.1 = ((s8[8388608]{0:T(1024)(128)(4,1)}), s8[4194304]{0:T(1024)(128)(4,1)S(1)}, s32[]{:S(2)}) async-start(s8[8388608]{0:T(1024)(128)(4,1)} %bitcast.58), calls=%async_computation.8 | async-start | bytes 8388608
  968.1 56.8 %slice-start.4 = ((s8[16777216]{0:T(1024)(128)(4,1)}), s8[4194304]{0:T(1024)(128)(4,1)S(1)}, s32[]{:S(2)}) async-start(s8[16777216]{0:T(1024)(128)(4,1)} %bitcast.64), calls=%async_computation.11 | async-start | bytes 8388608
  968.1 56.8 %slice-start.5 = ((s8[16777216]{0:T(1024)(128)(4,1)}), s8[4194304]{0:T(1024)(128)(4,1)S(1)}, s32[]{:S(2)}) async-start(s8[16777216]{0:T(1024)(128)(4,1)} %bitcast.64), calls=%async_computation.12 | async-start | bytes 8388608
Sparse Core Ops, SparseCore 0:
  9.5 37.1 all-gather.3
  48.9 227.2 all-gather.5
  336.0 49.5 all-reduce.3
  392.5 78.3 all-reduce.5
  685.4 147.0 reduce-scatter.1
  834.5 124.6 all-gather.7
where the time goes:
time: 1100 us; the launch traced here: 1090 us
  waiting for transfers between devices  626 us (57%)
  matrix products  253 us (23%)
  other arithmetic  132 us (12%)
  blocking collectives  43.3 us (4%)
  local copies, waits for them, and re-layouts  17.1 us (2%)
  between operations  17.1 us (2%)
    all_gather x1, waiting for transfers between devices, body(): lax.all_gather(activations, 'wide', axis=0, tiled=True)  229 us
    reduce_scatter x1, waiting for transfers between devices, body(): lax.psum_scatter(lax.dot_general(buffer, ortho_left, (((0,), (0,)), ((),...  147 us
    all_gather x1, waiting for transfers between devices, body(): right_raw = lax.all_gather(right_share, 'wide', axis=0, tiled=True)  82 us
    another operation x14, other arithmetic, body(): lower_factor = jnp.linalg.cholesky(gram_matrix)  78.6 us
    psum x1, waiting for transfers between devices, body(): gram_matrix = lax.psum(gram_local, 'wide')  78.3 us
    dot_general x1, matrix products, body(): lax.dot_general(ortho_left, right_raw, (((1,), (1,)), ((), ())), precisio...  57.3 us
    dot_general x1, matrix products, body(): lax.dot_general(ortho_left, new_right, (((1,), (1,)), ((), ())), precisio...  56.8 us
    dot_general x1, matrix products, body(): lax.dot_general(buffer, ortho_left, (((0,), (0,)), ((), ())), precision=h...  56.3 us
  transfers between devices with their start and end apart: 6, of which 6 were waited for; matrix products, arithmetic and copies ran while one was open for 0% of the time, Pallas kernels for 0%

commit v1 on v0

--- a/solution.py
+++ b/solution.py
@@ -44,7 +44,9 @@
         tiled=True,
     )
     col_squares = lax.psum(jnp.sum(right_share * right_share, axis=0), ("wide", "narrow"))
-    right_raw = lax.all_gather(right_share, "wide", axis=0, tiled=True)
+    right_raw = jnp.concatenate(
+        lax.all_to_all(jnp.stack([right_share] * lax.axis_size("wide")), "wide", 0, 0), axis=0
+    )
     feedback = lax.dot_general(
         ortho_left,
         right_raw,

time: 1100 us -> 1180 us (1.073)
  blocking collectives: 43.3 us -> 203 us
  waiting for transfers between devices: 626 us -> 544 us
    psum x1, blocking collectives: 43.3 us -> 203 us  [body(): lax.psum(jnp.sum(right_share * right_share, axis=0), ('wide', 'narrow'))]
    all_gather x1 -> x0, waiting for transfers between devices: 82 us -> none  [body(): right_raw = lax.all_gather(right_share, 'wide', axis=0, tiled=True)]
  transfers between devices with their start and end apart: 6 -> 6, of which waited for: 6 -> 5; matrix products, arithmetic and copies ran while one was open for 0% -> 0% of each run, Pallas kernels for 0% -> 0%
where the time goes in v1:
time: 1180 us; the launch traced here: 1170 us
  waiting for transfers between devices  544 us (46%)
  matrix products  252 us (21%)
  blocking collectives  203 us (17%)
  other arithmetic  126 us (11%)
  local copies, waits for them, and re-layouts  22.2 us (2%)
  between operations  16.7 us (1%)
    all_gather x1, waiting for transfers between devices, body(): lax.all_gather(activations, 'wide', axis=0, tiled=True)  229 us
    psum x1, blocking collectives, body(): lax.psum(jnp.sum(right_share * right_share, axis=0), ('wide', 'narrow'))  203 us
    reduce_scatter x1, waiting for transfers between devices, body(): lax.psum_scatter(lax.dot_general(buffer, ortho_left, (((0,), (0,)), ((),...  147 us
    another operation x14, other arithmetic, body(): lower_factor = jnp.linalg.cholesky(gram_matrix)  78.6 us
    psum x1, waiting for transfers between devices, body(): gram_matrix = lax.psum(gram_local, 'wide')  78.3 us
    dot_general x1, matrix products, body(): lax.dot_general(ortho_left, right_raw, (((1,), (1,)), ((), ())), precisio...  58.2 us
    dot_general x1, matrix products, body(): lax.dot_general(buffer, ortho_left, (((0,), (0,)), ((), ())), precision=h...  56.3 us
    dot_general x1, matrix products, body(): lax.dot_general(ortho_left, new_right, (((1,), (1,)), ((), ())), precisio...  54.3 us
  transfers between devices with their start and end apart: 6, of which 5 were waited for; matrix products, arithmetic and copies ran while one was open for 0% of the time, Pallas kernels for 0%

profile of v1, /device:TPU:0, one launch (start us, length us, event | category | flops | bytes accessed | tf_op | source)
XLA Modules:
  0.0 1169.5 jit_solution(12893448133682088445)
XLA Ops:
  8.7 38.1 %all-gather.3.cloned.1.call-done = bf16[2048,1024]{1,0:T(8,128)(2,1)} async-done(((bf16[512,1024]{1,0:T(8,128)(2,1)}), bf16[2048,1024]{1,0:T(8,128)(2,1)}) %all-gather.3.cloned.1.call-update) | async-done | bytes 4194320 | tf_op jit(solution)/shard_map/all_gather | solution.py:16
  46.7 229.4 %all-gather.5.cloned.1.call-done = bf16[2048,4096]{1,0:T(8,128)(2,1)} async-done(((bf16[256,4096]{1,0:T(8,128)(2,1)}), bf16[2048,4096]{1,0:T(8,128)(2,1)}) %all-gather.5.cloned.1.call-update) | async-done | bytes 16777232 | tf_op jit(solution)/shard_map/all_gather | solution.py:19
  276.2 28.3 %convolution_add_fusion = f32[1024,4096]{1,0:T(8,128)} fusion(f32[1024,4096]{1,0:T(8,128)} %param.6, bf16[2048,1024]{1,0:T(8,128)(2,1)} %all-gather.3.cloned.1.call-done, bf16[2048,4096]{1,0:T(8,128)(2,1)} %all-gather.5.cloned.1.call-done), kind=kOutput, calls=%fused_computation.4 | convolution fusion | flops 17184063488 | bytes 54525952 | tf_op jit(solution)/shard_map/dot_general | solution.py:17
  304.5 31.4 %fusion.39 = f32[1024,512]{1,0:T(8,128)} fusion(f32[1024,4096]{1,0:T(8,128)} %convolution_add_fusion, f32[4096,512]{1,0:T(8,128)} %param.7), kind=kOutput, calls=%fused_computation.78 | convolution fusion | flops 25769803776 | bytes 27262976 | tf_op jit(solution)/shard_map/dot_general | solution.py:24
  336.0 49.7 %all-reduce.4.cloned.1.call-done = f32[1024,512]{1,0:T(8,128)} async-done(((f32[1024,512]{1,0:T(8,128)}), f32[1024,512]{1,0:T(8,128)}) %all-reduce.4.cloned.1.call-update) | async-done | bytes 2097168 | tf_op jit(solution)/shard_map/psum | solution.py:27
  385.6 6.7 fusion.40
  392.6 78.3 %all-reduce.6.cloned.1.call-done = f32[512,512]{0,1:T(8,128)} async-done(((f32[512,512]{0,1:T(8,128)}), f32[512,512]{0,1:T(8,128)}) %all-reduce.6.cloned.1.call-update) | async-done | bytes 1048592 | tf_op jit(solution)/shard_map/psum | solution.py:31
  474.9 11.7 %cholesky.104 = f32[128,128]{1,0:T(8,128)S(1)} custom-call(f32[128,128]{1,0:T(8,128)S(1)} %cholesky.266), custom_call_target="Cholesky" | custom-call | tf_op jit(solution)/shard_map/jit(cholesky)/cholesky | solution.py:32
  486.8 9.8 custom-call.31
  499.1 11.7 %cholesky.217 = f32[128,128]{1,0:T(8,128)S(1)} custom-call(f32[128,128]{1,0:T(8,128)S(1)} %cholesky.270), custom_call_target="Cholesky" | custom-call | tf_op jit(solution)/shard_map/jit(cholesky)/cholesky | solution.py:32
  510.9 10.0 custom-call.32
  522.5 11.7 %cholesky.238 = f32[128,128]{1,0:T(8,128)S(1)} custom-call(f32[128,128]{1,0:T(8,128)S(1)} %cholesky.275), custom_call_target="Cholesky" | custom-call | tf_op jit(solution)/shard_map/jit(cholesky)/cholesky | solution.py:32
  534.2 9.8 custom-call.33
  545.5 11.7 %cholesky.255 = f32[128,128]{1,0:T(8,128)S(1)} custom-call(f32[128,128]{1,0:T(8,128)S(1)} %convolution_subtract_fusion.4), custom_call_target="Cholesky" | custom-call | tf_op jit(solution)/shard_map/jit(cholesky)/cholesky | solution.py:32
  563.2 13.8 %while.1 = (s32[]{:T(128)}, f32[512,512]{1,0:T(8,128)}, s32[4,2]{0,1:T(2,128)S(1)}, f32[4,128,128]{2,1,0:T(8,128)}, s32[]{:T(128)}) while((s32[]{:T(128)}, f32[512,512]{1,0:T(8,128)}, s32[4,2]{0,1:T(2,128)S(1)}, f32[4,128,128]{2,1,0:T(8,128)}, s32[]{:T(128)}) %tuple.31), condition=%wide.while_cond, body=%wide.while_body.sunk | while | flops 2 | bytes 132205 | solution.py:33
  577.1 40.1 %custom-call.34 = f32[4,128,128]{1,2,0:T(8,128)S(1)} custom-call(f32[4,128,128]{2,1,0:T(8,128)} %get-tuple-element.10), custom_call_target="InvertDiagBlocksLowerTriangular" | custom-call | tf_op jit(solution)/shard_map/jit(_solve_triangular)/triangular_solve | solution.py:33
  628.2 56.3 %fusion.15 = f32[4096,512]{1,0:T(8,128)} fusion(f32[1024,4096]{1,0:T(8,128)} %convolution_add_fusion, f32[128,1024]{1,0:T(8,128)S(1)} %fusion.24, f32[128,1024]{1,0:T(8,128)S(1)} %fusion.25, f32[128,1024]{1,0:T(8,128)S(1)} %fusion.27, f32[128,1024]{1,0:T(8,128)S(1)} %fusion.13), kind=kOutput, calls=%fused_computation.31 | convolution fusion | flops 25771376640 | bytes 27262976 | tf_op jit(solution)/shard_map/dot_general | solution.py:35
  684.5 147.2 %reduce-scatter.2.cloned.1.call-done = f32[512,512]{1,0:T(8,128)} async-done(((f32[4096,512]{1,0:T(8,128)}), f32[512,512]{1,0:T(8,128)}) %reduce-scatter.2.cloned.1.call-update) | async-done | bytes 1048592 | tf_op jit(solution)/shard_map/reduce_scatter | solution.py:34
  831.7 5.7 stack.2
  837.4 5.1 all-to-all-start
  842.7 203.1 %psum.23 = f32[512]{0:T(512)S(1)} all-reduce(f32[512]{0:T(512)S(1)} %multiply_reduce_fusion), channel_id=1, replica_groups=mesh['wide'=8,'narrow'=4] {'wide','narrow'}, use_global_device_ids=true, to_apply=%region_12.13 | all-reduce | flops 512 | bytes 4096 | tf_op jit(solution)/shard_map/psum | solution.py:46
  1045.8 58.2 %multiply_subtract_fusion = f32[1024,4096]{1,0:T(8,128)} fusion(f32[1024,4096]{1,0:T(8,128)} %convolution_add_fusion, f32[4096,512]{1,0:T(8,128)} %bitcast.12, f32[128,1024]{1,0:T(8,128)S(1)} %fusion.24, f32[128,1024]{1,0:T(8,128)S(1)} %copy-done.3, f32[128,1024]{1,0:T(8,128)S(1)} %fusion.27, f32[128,1024]{1,0:T(8,128)S(1)} %fusion.13), kind=kOutput, calls=%fused_computation.3 | convolution fusion | flops 25779765248 | bytes 44040192 | tf_op jit(solution)/shard_map/dot_general | solution.py:50
  1104.0 4.4 broadcast_divide_fusion
  1108.5 54.3 %multiply_convert_fusion = bf16[1024,4096]{1,0:T(8,128)(2,1)} fusion(f32[4096,512]{1,0:T(8,128)S(1)} %broadcast_divide_fusion, f32[128,1024]{1,0:T(8,128)S(1)} %fusion.24, f32[128,1024]{1,0:T(8,128)S(1)} %copy-done.3, f32[128,1024]{1,0:T(8,128)S(1)} %fusion.27, f32[128,1024]{1,0:T(8,128)S(1)} %fusion.13), kind=kOutput, calls=%fused_computation.2 | convolution fusion | flops 25779765248 | bytes 18874368 | tf_op jit(solution)/shard_map/dot_general | solution.py:60
  (67 shorter events, 40.0 us)
Async XLA Ops:
  7.2 39.6 %all-gather.3.cloned.1.call-start = ((), (), s32[]{:S(2)}) async-start(), calls=%async_computation.2 | async-start | bytes 5242880 | tf_op jit(solution)/shard_map/all_gather | solution.py:16
  7.9 268.3 %all-gather.5.cloned.1.call-start = ((), (), s32[]{:S(2)}) async-start(), calls=%async_computation.3 | async-start | bytes 18874368 | tf_op jit(solution)/shard_map/all_gather | solution.py:19
  8.6 377.0 %all-reduce.4.cloned.1.call-start = ((), (), s32[]{:S(2)}) async-start(), calls=%async_computation.4 | async-start | bytes 4194304 | tf_op jit(solution)/shard_map/psum | solution.py:27
  335.9 135.0 %all-reduce.6.cloned.1.call-start = ((), (), s32[]{:S(2)}) async-start(), calls=%async_computation.5 | async-start | bytes 2097152 | tf_op jit(solution)/shard_map/psum | solution.py:31
  392.4 439.4 %reduce-scatter.2.cloned.1.call-start = ((), (), s32[]{:S(2)}) async-start(), calls=%async_computation.6 | async-start | bytes 9437184 | tf_op jit(solution)/shard_map/reduce_scatter | solution.py:34
  473.9 1.0 copy-start.5
  474.9 142.3 %copy-start = (f32[1024,512]{1,0:T(8,128)S(1)}, f32[1024,512]{1,0:T(8,128)}, u32[]{:S(2)}) copy-start(f32[1024,512]{1,0:T(8,128)} %all-reduce.4.cloned.1.call-done) | copy-start | bytes 6291460
  623.7 4.5 copy-start.2
  837.4 5.1 copy-start.4
  837.4 208.3 %copy-start.3 = (f32[128,1024]{1,0:T(8,128)S(1)}, f32[128,1024]{1,0:T(8,128)}, u32[]{:S(2)}) copy-start(f32[128,1024]{1,0:T(8,128)} %copy-done.2) | copy-start | bytes 1572868
  837.4 208.3 %all-to-all-start = ((f32[8,512,512]{2,1,0:T(8,128)}), f32[8,512,512]{2,1,0:T(8,128)}, u32[]{:S(2)}, u32[]{:S(2)}) async-start(f32[8,512,512]{2,1,0:T(8,128)} %stack.2), calls=%async_computation.1 | async-start | bytes 16777216 | tf_op jit(solution)/shard_map/all_to_all | solution.py:48
  1108.5 54.3 %copy-start.1 = (f32[4096,512]{1,0:T(8,128)}, f32[4096,512]{1,0:T(8,128)S(1)}, u32[]{:S(2)}) copy-start(f32[4096,512]{1,0:T(8,128)S(1)} %broadcast_divide_fusion) | copy-start | bytes 25165828
Sparse Core Ops, SparseCore 0:
  9.5 37.1 all-gather.2
  48.9 227.2 all-gather.4
  336.0 49.5 all-reduce.3
  392.5 78.3 all-reduce.5
  684.7 147.0 reduce-scatter.1
